TPU v7x, 64 devices: a 2x2x8 block of a 4x4x8 slice. The times are simulated.
64 devices in a mesh: dp: 4 (over x, y), vp: 16 (over z, core).
Axes of the slice: x: 2, y: 2, z: 8, core: 2. Of those that a mesh axis runs over, the one named last changes fastest.
The devices are a block of a 4x4x8 slice.
Arguments:
- hidden: bfloat16 [256, 128, 768], P('vp', 'dp'), parts along dimension 1
- norm_gain: float32 [768], replicated
- norm_bias: float32 [768], replicated
- w_out: bfloat16 [768, 51200], P(None, 'vp')
- labels: int32 [256, 128], P('vp', 'dp'), parts along dimension 1
- loss_mask: float32 [256, 128], P('vp', 'dp'), parts along dimension 1
Outputs:
- output 1: float32 [4], P('dp'), parts along dimension 0
- output 2: bfloat16 [256, 128, 768], P('vp', 'dp'), parts along dimension 1
- output 3: float32 [3072, 51200], P('dp', 'vp'), parts along dimension 0
- output 4: float32 [3072], P('dp'), parts along dimension 0
- output 5: float32 [3072], P('dp'), parts along dimension 0
There are 4 independent parts. A program takes and returns all parts, laid end to end along the dimension named above; an argument that names none is the same for every part.
All inputs are finite; a program needn't handle non-finite values.
Results may differ from a plain program's by a relative error of at most 0.001.
Values are sent between devices in bfloat16 or wider.
A program may use at most 768 MiB of HBM per device.

v0:
```python
import jax
import jax.numpy as jnp
from jax import lax
from jax.sharding import PartitionSpec as P

NORM_EPS = 1e-5


def norm_forward(hidden, norm_gain, norm_bias):
    x_float = hidden.astype(jnp.float32)
    tok_mean = jnp.mean(x_float, axis=-1, keepdims=True)
    centered = x_float - tok_mean
    inv_std = lax.rsqrt(jnp.mean(centered * centered, axis=-1, keepdims=True) + NORM_EPS)
    normed = centered * inv_std
    h_bf = (normed * (1.0 + norm_gain) + norm_bias).astype(jnp.bfloat16)
    return h_bf, normed, inv_std


def norm_backward(grad_h, normed, inv_std, norm_gain):
    scaled = grad_h * (1.0 + norm_gain)
    centered_grad = scaled - jnp.mean(scaled, axis=-1, keepdims=True)
    return (inv_std * (centered_grad - normed * jnp.mean(scaled * normed, axis=-1, keepdims=True))).astype(jnp.bfloat16)


def solution(mesh):
    def per_device(hidden, norm_gain, norm_bias, w_blk, labels, loss_mask):
        h_bf, normed, inv_std = norm_forward(hidden, norm_gain, norm_bias)
        h_all = lax.all_gather(h_bf, "vp", axis=0, tiled=True)
        labels_all = lax.all_gather(labels, "vp", axis=0, tiled=True)
        mask_all = lax.all_gather(loss_mask, "vp", axis=0, tiled=True)
        vocab_local = w_blk.shape[1]
        col_start = lax.axis_index("vp") * vocab_local
        logits = jnp.einsum("sbd,dv->sbv", h_all, w_blk, preferred_element_type=jnp.float32)
        row_max = lax.pmax(jnp.max(logits, axis=-1), "vp")
        exp_shift = jnp.exp(logits - row_max[:, :, None])
        col_ids = col_start + lax.broadcasted_iota(jnp.int32, (1, 1, vocab_local), 2)
        is_label = col_ids == labels_all[:, :, None]
        sum_exp = lax.psum(jnp.sum(exp_shift, axis=-1), "vp")
        target = lax.psum(jnp.sum(jnp.where(is_label, logits, 0.0), axis=-1), "vp")
        mask_total = jnp.sum(mask_all)
        tok_loss = row_max + jnp.log(sum_exp) - target
        loss = jnp.sum(mask_all * tok_loss) / mask_total
        prob_soft = exp_shift / sum_exp[:, :, None]
        tok_weight = mask_all / mask_total
        grad_logits = (jnp.where(is_label, prob_soft - 1.0, prob_soft) * tok_weight[:, :, None]).astype(jnp.bfloat16)
        grad_w = jnp.einsum("sbd,sbv->dv", h_all, grad_logits, preferred_element_type=jnp.float32)
        grad_h_part = jnp.einsum("sbv,dv->sbd", grad_logits, w_blk, preferred_element_type=jnp.float32)
        grad_h = lax.psum_scatter(grad_h_part, "vp", scatter_dimension=0, tiled=True)
        grad_gain = lax.psum(jnp.sum(grad_h * normed, axis=(0, 1)), "vp")
        grad_bias = lax.psum(jnp.sum(grad_h, axis=(0, 1)), "vp")
        grad_x = norm_backward(grad_h, normed, inv_std, norm_gain)
        return loss.reshape(1), grad_x, grad_w, grad_gain, grad_bias

    tok_spec = P("vp", "dp")
    return jax.shard_map(
        per_device,
        mesh=mesh,
        in_specs=(P("vp", "dp", None), P(None), P(None), P(None, "vp"), tok_spec, tok_spec),
        out_specs=(P("dp"), P("vp", "dp", None), P("dp", "vp"), P("dp"), P("dp")),
        check_vma=False,
    )
```

profile of v0, /device:TPU:21, one launch (start us, length us, event | category | flops | bytes accessed | tf_op | source)
XLA Modules:
  0.0 572.8 jit_solution(4644194727941331114)
XLA Ops:
  7.2 0.1 all-gather.2.cloned.1.call-start
  7.2 0.7 broadcast_add_fusion
  7.9 0.0 copy-start.8
  7.9 1.6 convert_reduce_fusion
  9.6 0.0 copy-start.1
  9.6 1.7 fusion.21
  11.3 0.0 copy-done.8
  11.3 0.0 copy-done.1
  11.3 0.0 copy-start.5
  11.3 0.6 copy-done.5
  11.9 2.6 fusion.15
  14.5 0.1 all-gather.2.cloned.1.call-update
  14.6 0.1 reduce-scatter.2.cloned.1.call-start
  14.7 23.4 %all_gather.9 = f32[256,32]{1,0:T(8,128)S(1)} all-gather(f32[16,32]{1,0:T(8,128)} %param.11), channel_id=1, replica_groups=mesh['dp'=4,'vp'=16] {'vp'}, dimensions={0}, use_global_device_ids=true | all-gather | bytes 34816 | tf_op jit(solution)/shard_map/all_gather | solution.py:30
  38.1 0.1 copy.28
  38.1 0.0 copy-start.3
  38.1 0.6 reduce_sum.95
  38.8 15.6 %all_gather.11 = s32[256,32]{1,0:T(8,128)S(1)} all-gather(s32[16,32]{1,0:T(8,128)} %param.10), channel_id=1, replica_groups=mesh['dp'=4,'vp'=16] {'vp'}, dimensions={0}, use_global_device_ids=true | all-gather | bytes 34816 | tf_op jit(solution)/shard_map/all_gather | solution.py:29
  54.3 0.1 copy.27
  54.4 0.7 broadcast_divide_fusion
  55.1 37.9 %all-gather.2.cloned.1.call-done = bf16[256,32,768]{2,0,1:T(8,128)(2,1)} async-done(((bf16[16,32,768]{2,0,1:T(8,128)(2,1)}), bf16[256,32,768]{2,0,1:T(8,128)(2,1)}) %all-gather.2.cloned.1.call-update) | async-done | bytes 12582928 | tf_op jit(solution)/shard_map/all_gather | solution.py:28
  93.0 55.0 %fusion.22 = (f32[256,32]{0,1:T(8,128)S(1)}, f32[256,32,3200]{2,0,1:T(8,128)}) fusion(bf16[256,32,768]{2,0,1:T(8,128)(2,1)} %all-gather.2.cloned.1.call-done, bf16[768,3200]{1,0:T(8,128)(2,1)} %param.9), kind=kOutput, calls=%fused_computation.37 | convolution fusion | flops 40291524608 | bytes 122388480 | tf_op jit(solution)/shard_map/sbd,dv->sbv/dot_general | solution.py:33
  148.0 0.0 copy-done.3
  148.0 43.6 %pmax.7 = f32[256,32]{0,1:T(8,128)S(1)} all-reduce(f32[256,32]{0,1:T(8,128)S(1)} %get-tuple-element.34), channel_id=1, replica_groups=mesh['dp'=4,'vp'=16] {'vp'}, use_global_device_ids=true, to_apply=%region_3.0 | all-reduce | flops 8192 | bytes 65536 | tf_op jit(solution)/shard_map/pmax | solution.py:34
  191.6 33.1 %fusion.3 = (f32[256,32]{0,1:T(8,128)S(1)}, f32[256,32]{0,1:T(8,128)}) fusion(f32[256,32,3200]{2,0,1:T(8,128)} %get-tuple-element.35, f32[256,32]{0,1:T(8,128)S(1)} %pmax.7, s32[256,32]{0,1:T(8,128)S(1)} %copy.27, s32[3200]{0:T(1024)S(1)} %iota_add_fusion), kind=kLoop, calls=%fused_computation.6 | loop fusion | flops 131055616 | bytes 105001472 | tf_op jit(solution)/shard_map/reduce_sum | solution.py:38
  224.7 45.9 %psum.28 = f32[256,32]{0,1:T(8,128)S(1)} all-reduce(f32[256,32]{0,1:T(8,128)S(1)} %get-tuple-element.25), channel_id=1, replica_groups=mesh['dp'=4,'vp'=16] {'vp'}, use_global_device_ids=true, to_apply=%region_5.0 | all-reduce | flops 8192 | bytes 65536 | tf_op jit(solution)/shard_map/psum | solution.py:38
  270.6 50.9 %fusion.2 = bf16[256,32,3200]{2,0,1:T(8,128)(2,1)} fusion(f32[256,32,3200]{2,0,1:T(8,128)} %get-tuple-element.35, f32[256,32]{0,1:T(8,128)S(1)} %broadcast_divide_fusion, f32[256,32]{0,1:T(8,128)S(1)} %psum.28, s32[256,32]{0,1:T(8,128)S(1)} %copy.27, s32[3200]{0:T(1024)S(1)} %iota_add_fusion, f32[256,32]{0,1:T(8,128)S(1)} %pmax.7), kind=kLoop, calls=%fused_computation.4 | loop fusion | flops 183500800 | bytes 157430272 | tf_op jit(solution)/shard_map/convert_element_type | solution.py:45
  321.5 49.7 %fusion.4 = f32[256,32,768]{2,0,1:T(8,128)} fusion(bf16[256,32,3200]{2,0,1:T(8,128)(2,1)} %fusion.2, bf16[768,3200]{1,0:T(8,128)(2,1)} %param.9), kind=kOutput, calls=%fused_computation.8 | convolution fusion | flops 40265318400 | bytes 82509824 | tf_op jit(solution)/shard_map/sbv,dv->sbd/dot_general | solution.py:47
  371.2 0.1 reduce-scatter.2.cloned.1.call-update
  371.3 0.0 copy-start
  371.3 0.0 copy-start.2
  371.3 0.0 copy-start.6
  371.3 0.0 copy-start.9
  371.3 0.0 copy-start.7
  371.4 0.0 copy-start.4
  371.4 51.7 %convolution_bitcast_fusion = f32[768,3200]{1,0:T(8,128)} fusion(bf16[256,32,768]{2,0,1:T(8,128)(2,1)} %all-gather.2.cloned.1.call-done, bf16[256,32,3200]{2,0,1:T(8,128)(2,1)} %fusion.2), kind=kOutput, calls=%fused_computation.7 | convolution fusion | flops 40265318400 | bytes 74842112 | tf_op jit(solution)/shard_map/sbd,sbv->dv/dot_general | solution.py:46
  423.0 89.8 %reduce-scatter.2.cloned.1.call-done = f32[16,32,768]{2,0,1:T(8,128)} async-done(((f32[256,32,768]{2,0,1:T(8,128)}), f32[16,32,768]{2,0,1:T(8,128)}) %reduce-scatter.2.cloned.1.call-update) | async-done | bytes 1572880 | tf_op jit(solution)/shard_map/reduce_scatter | solution.py:48
  512.9 0.0 copy-done
  512.9 0.0 copy-done.2
  512.9 0.0 copy-done.6
  512.9 0.0 copy-done.9
  512.9 2.5 fusion.20
  515.4 0.0 copy-done.7
  515.4 44.2 %all-reduce = (f32[256,32]{0,1:T(8,128)S(1)}, f32[768]{0:T(1024)}, f32[768]{0:T(1024)}) all-reduce(f32[256,32]{0,1:T(8,128)S(1)} %copy-done.7, f32[768]{0:T(1024)S(1)} %get-tuple-element.27, f32[768]{0:T(1024)S(1)} %get-tuple-element.30), channel_id=1, replica_groups=mesh['dp'=4,'vp'=16] {'vp'}, use_global_device_ids=true, to_apply=%region_7.8 | all-reduce | flops 9728 | bytes 77824 | tf_op jit(solution)/shard_map/psum | solution.py:39
  559.6 0.0 copy-done.4
  559.6 0.6 multiply_reduce_fusion.1
  561.6 2.2 fusion.19
  563.7 1.1 copy.30
  (4 shorter events, 0.0 us)
Async XLA Ops:
  7.2 85.8 %all-gather.2.cloned.1.call-start = ((), (), s32[]{:S(2)}) async-start(), calls=%async_computation.1 | async-start | bytes 13369344 | tf_op jit(solution)/shard_map/all_gather | solution.py:28
  7.9 3.4 copy-start.8
  9.6 1.7 copy-start.1
  11.3 0.6 copy-start.5
  14.6 498.3 %reduce-scatter.2.cloned.1.call-start = ((), (), s32[]{:S(2)}) async-start(), calls=%async_computation.2 | async-start | bytes 26738688 | tf_op jit(solution)/shard_map/reduce_scatter | solution.py:48
  38.1 109.9 %copy-start.3 = (f32[256,32]{0,1:T(8,128)}, f32[256,32]{0,1:T(8,128)S(1)}, u32[]{:S(2)}) copy-start(f32[256,32]{0,1:T(8,128)S(1)} %copy.28) | copy-start | bytes 98308
  371.3 141.6 %copy-start = (bf16[16,32,768]{2,1,0:T(8,128)(2,1)S(1)}, bf16[16,32,768]{2,1,0:T(8,128)(2,1)}, u32[]{:S(2)}) copy-start(bf16[16,32,768]{2,1,0:T(8,128)(2,1)} %param.6) | copy-start | bytes 2359300
  371.3 141.6 %copy-start.2 = (f32[16,32]{0,1:T(8,128)S(1)}, f32[16,32]{0,1:T(8,128)}, u32[]{:S(2)}) copy-start(f32[16,32]{0,1:T(8,128)} %copy-done.1) | copy-start | bytes 6148
  371.3 141.6 %copy-start.6 = (f32[16,32]{0,1:T(8,128)S(1)}, f32[16,32]{0,1:T(8,128)}, u32[]{:S(2)}) copy-start(f32[16,32]{0,1:T(8,128)} %copy-done.5) | copy-start | bytes 6148
  371.3 141.5 %copy-start.9 = (f32[768]{0:T(1024)S(1)}, f32[768]{0:T(1024)}, u32[]{:S(2)}) copy-start(f32[768]{0:T(1024)} %copy-done.8) | copy-start | bytes 9220
  371.3 144.0 %copy-start.7 = (f32[256,32]{0,1:T(8,128)S(1)}, f32[256,32]{0,1:T(8,128)}, u32[]{:S(2)}) copy-start(f32[256,32]{0,1:T(8,128)} %get-tuple-element.26) | copy-start | bytes 98308
  371.4 188.2 %copy-start.4 = (f32[256,32]{0,1:T(8,128)S(1)}, f32[256,32]{0,1:T(8,128)}, u32[]{:S(2)}) copy-start(f32[256,32]{0,1:T(8,128)} %copy-done.3) | copy-start | bytes 98308
Sparse Core Ops, SparseCore 0:
  14.7 78.2 all-gather.1
  371.4 141.4 reduce-scatter.1
where the time goes:
time: 575 us; the launch traced here: 573 us
  blocking collectives  173 us (30%)
  matrix products  156 us (27%)
  waiting for transfers between devices  128 us (22%)
  other arithmetic  97.2 us (17%)
  between operations  16.7 us (3%)
    reduce_scatter x1, waiting for transfers between devices, per_device(): lax.psum_scatter(grad_h_part, 'vp', scatter_dimension=0, tiled=True)  89.8 us
    dot_general x1, matrix products, per_device(): jnp.einsum('sbd,dv->sbv', h_all, w_blk, preferred_element_type=jnp.float32)  55 us
    dot_general x1, matrix products, per_device(): jnp.einsum('sbd,sbv->dv', h_all, grad_logits, preferred_element_type=jnp....  51.7 us
    convert_element_type x1, other arithmetic, per_device(): (jnp.where(is_label, prob_soft - 1.0, prob_soft) * tok_weight[:, :, None]...  50.9 us
    dot_general x1, matrix products, per_device(): jnp.einsum('sbv,dv->sbd', grad_logits, w_blk, preferred_element_type=jnp....  49.7 us
    psum x1, blocking collectives, per_device(): sum_exp = lax.psum(jnp.sum(exp_shift, axis=-1), 'vp')  45.9 us
    psum x1, blocking collectives, per_device(): target = lax.psum(jnp.sum(jnp.where(is_label, logits, 0.0), axis=-1), 'vp')  44.2 us
    pmax x1, blocking collectives, per_device(): row_max = lax.pmax(jnp.max(logits, axis=-1), 'vp')  43.6 us
  transfers between devices with their start and end apart: 2, of which 2 were waited for; matrix products, arithmetic and copies ran while one was open for 9% of the time, Pallas kernels for 0%

commit v1 on v0

v1 whole, which is shorter than its diff:
```python
import functools

import jax
import jax.numpy as jnp
from jax import lax
from jax.experimental import pallas as pl
from jax.experimental.pallas import tpu as pltpu
from jax.sharding import PartitionSpec as P

NORM_EPS = 1e-5
F32 = jnp.float32
BF16 = jnp.bfloat16
MESH = pl.DeviceIdType.MESH


def row_chunk(rows, limit):
    best = 16
    for size in range(16, limit + 1, 16):
        if rows % size == 0:
            best = size
    return best


def head_kernel(
    n, x_ref, gain_ref, bias_ref, w_hbm, aux_ref,
    dx_ref, dwt_hbm, dgain_ref, dbias_ref, loss_ref, z_hbm,
    w_v, wt, h_all, dw_acc, zbuf, dzb, h_pair, own, give, ring_in, mate_in,
    aux_all, st_loc, st_all, lse_all, t_acc, fin_all,
    w_sem, dw_sem, z_sem,
    f_send, f_recv, p_send, p_recv,
    a_send, a_recv, s_send, s_recv, l_send, l_recv, e_send, e_recv,
    r_send, r_recv, q_send, q_recv, r_cred, q_cred,
):
    chips = n // 2
    me = lax.axis_index("vp")
    zc, core = me // 2, me % 2
    mate = zc * 2 + 1 - core
    up = lax.rem(zc + 1, chips) * 2 + core
    down = lax.rem(zc + chips - 1, chips) * 2 + core
    ahead = (up, down)
    depth, cols = w_v.shape
    half = x_ref.shape[0] // 2
    sub = half // 2
    vchunk = row_chunk(cols, 640)
    col_start = me * cols

    def remote(src, dst, send, recv, dev):
        return pltpu.make_async_remote_copy(
            src_ref=src, dst_ref=dst, send_sem=send, recv_sem=recv,
            device_id={"vp": dev}, device_id_type=MESH)

    def peer_of(k):
        return lax.rem(me + k, n)

    w_copy = pltpu.make_async_copy(w_hbm, w_v, w_sem)
    w_copy.start()

    barrier = pltpu.get_barrier_semaphore()
    for k in range(1, n):
        pl.semaphore_signal(barrier, inc=1, device_id={"vp": peer_of(k)}, device_id_type=MESH)

    gain = 1.0 + gain_ref[...]
    bias = bias_ref[...]

    def normed_rows(rows):
        xf = rows.astype(F32)
        centered = xf - jnp.mean(xf, axis=-1, keepdims=True)
        inv_std = lax.rsqrt(jnp.mean(centered * centered, axis=-1, keepdims=True) + NORM_EPS)
        return centered * inv_std, inv_std

    ln_rows = half // 4

    @pl.loop(0, 8)
    def _(i):
        row0 = pl.multiple_of((i % 4) * ln_rows, ln_rows)
        src0 = pl.multiple_of(i * ln_rows, ln_rows)
        normed, _ = normed_rows(x_ref[pl.ds(src0, ln_rows), :])
        h_all[me, i // 4, pl.ds(row0, ln_rows), :] = (normed * gain + bias).astype(BF16)

    aux_all[me] = aux_ref[...]
    t_acc[...] = jnp.zeros_like(t_acc)
    pl.semaphore_wait(barrier, n - 1)

    def ring_copy(d, k, blk, hf):
        ref = h_all.at[blk, hf]
        return remote(ref, ref, f_send.at[d, k], f_recv.at[d, k], ahead[d])

    def mate_copy(d, k, blk, hf):
        ref = h_all.at[blk, hf]
        return remote(ref, ref, p_send.at[d, k], p_recv.at[d, k], mate)

    def fwd_half(d, k):
        return (k + 1) % 2 if d == 0 else k % 2

    for k in (1, 2):
        for d in (0, 1):
            ring_copy(d, k, me, fwd_half(d, k)).start()

    def spread(ref, dst, send, recv):
        for k in range(1, n):
            remote(ref, dst, send.at[k], recv.at[me], peer_of(k)).start()

    def collect(ref_all, send, recv):
        for k in range(1, n):
            src = peer_of(k)
            remote(ref_all.at[src], ref_all.at[src], send.at[k], recv.at[src], src).wait_recv()

    def drain(ref, send, recv):
        for k in range(1, n):
            remote(ref, ref, send.at[k], recv.at[me], peer_of(k)).wait_send()

    spread(aux_all.at[me], aux_all.at[me], a_send, a_recv)

    w_copy.wait()
    tcols = 128 if cols % 128 == 0 else cols

    @pl.loop(0, cols // tcols)
    def _(i):
        c0 = pl.multiple_of(i * tcols, tcols)
        wt[pl.ds(c0, tcols), :] = w_v[:, pl.ds(c0, tcols)].T

    @pl.loop(0, cols // vchunk)
    def _(i):
        c0 = pl.multiple_of(i * vchunk, vchunk)
        dw_acc[pl.ds(c0, vchunk), :] = jnp.zeros((vchunk, depth), F32)

    last = chips - 1

    def z_out(slot, tile):
        return pltpu.make_async_copy(zbuf.at[slot], z_hbm.at[tile], z_sem.at[slot])

    def fwd_chip(d, k):
        step = (k + 1) // 2
        return lax.rem(zc + chips - step, chips) if d == 0 else lax.rem(zc + step, chips)

    @pl.loop(0, chips)
    def _(k):
        for d in (0, 1):
            blk = fwd_chip(d, k) * 2 + core
            hf = fwd_half(d, k)

            @pl.when(k >= 1)
            def _():
                ring_copy(d, k, blk, hf).wait_recv()

                @pl.when(k + 2 <= last)
                def _():
                    ring_copy(d, k + 2, blk, hf).start()

            mate_copy(d, k, blk, hf).start()

        @pl.loop(0, 4)
        def _(q):
            d = q % 2
            step = (k + 1) // 2
            chip = lax.rem(zc + 2 * chips + (2 * d - 1) * step, chips)
            hf = lax.rem(k + 1 + d, 2)
            blk = chip * 2 + jnp.where(q < 2, core, 1 - core)

            @pl.when(q >= 2)
            def _():
                mate_copy(d, k, blk, hf).wait_recv()

            slot = d

            @pl.when(k * 4 + q >= 2)
            def _():
                z_out(slot, 0).wait()

            m8 = jnp.full((8, half), -jnp.inf, F32)
            s8 = jnp.zeros((8, half), F32)
            h_tile = h_all[blk, hf]
            for j in range(cols // vchunk):
                rows = pl.ds(j * vchunk, vchunk)
                z = lax.dot_general(wt[rows, :], h_tile, (((1,), (1,)), ((), ())), preferred_element_type=F32)
                zbuf[slot, rows, :] = z
                z3 = z.reshape(vchunk // 8, 8, half)
                m_new = jnp.maximum(m8, jnp.max(z3, axis=0))
                s8 = s8 * jnp.exp(m8 - m_new) + jnp.sum(jnp.exp(z3 - m_new[None]), axis=0)
                m8 = m_new
            m1 = jnp.max(m8, axis=0, keepdims=True)
            st_loc[blk, hf, 0:1, :] = m1
            st_loc[blk, hf, 1:2, :] = jnp.sum(s8 * jnp.exp(m8 - m1), axis=0, keepdims=True)
            z_out(slot, blk * 2 + hf).start()

    z_out(0, 0).wait()
    z_out(1, 0).wait()

    def bwd_place(j):
        d, s = lax.rem(j, 2), j // 2
        chip = lax.rem(zc + 2 * chips + (2 * d - 1) * (s + 1), chips)
        return d, s, chip

    def z_in(slot, j):
        d, _, chip = bwd_place(j)
        blk = chip * 2 + (core if slot == 0 else 1 - core)
        return pltpu.make_async_copy(z_hbm.at[blk * 2 + d], zbuf.at[slot], z_sem.at[slot])

    z_in(0, 0).start()
    z_in(1, 0).start()

    for k in range(1, n):
        peer = peer_of(k)
        remote(st_loc.at[peer], st_all.at[me], s_send.at[k], s_recv.at[me], peer).start()
    st_all[me] = st_loc[me]
    collect(st_all, s_send, s_recv)
    for hf in (0, 1):
        tops = [st_all[i, hf, 0:1, :] for i in range(n)]
        top = functools.reduce(jnp.maximum, tops)
        total = functools.reduce(jnp.add, [st_all[i, hf, 1:2, :] * jnp.exp(tops[i] - top) for i in range(n)])
        lse_all[me, hf] = top + jnp.log(total)
    spread(lse_all.at[me], lse_all.at[me], l_send, l_recv)
    collect(aux_all, a_send, a_recv)
    mask_sum = functools.reduce(jnp.add, [aux_all[i, hf, 1:2, :] for i in range(n) for hf in (0, 1)])
    mask_total = jnp.sum(mask_sum, axis=1, keepdims=True)
    collect(lse_all, l_send, l_recv)

    def ring_sum(d, slot, sb):
        return remote(own.at[d, slot, sb], ring_in.at[d, slot, sb], r_send.at[d, slot, sb], r_recv.at[d, slot, sb],
                      jnp.where(d == 0, up, down))

    def mate_sum(d, slot):
        return remote(give.at[d, slot], mate_in.at[d, slot], q_send.at[d, slot], q_recv.at[d, slot], mate)

    def event(j, sb):
        d, s, _ = bwd_place(j)
        slot = lax.rem(s, 2)
        prev = lax.rem(s + 1, 2)
        if sb == 0:
            mate_sum(d, slot).wait_recv()

        @pl.when(s == 0)
        def _():
            own[d, slot, sb] = own[d, slot, sb] + mate_in[d, slot, sb]

        @pl.when(s >= 1)
        def _():
            ring_sum(d, prev, sb).wait_recv()
            own[d, slot, sb] = (own[d, slot, sb] + mate_in[d, slot, sb]) + ring_in[d, prev, sb]

        @pl.when(s <= chips - 2)
        def _():
            if sb == 0:
                @pl.when(s >= 2)
                def _():
                    pl.semaphore_wait(r_cred.at[d], 1)
            ring_sum(d, slot, sb).start()

        if sb == 1:
            @pl.when((s >= 1) & (s <= chips - 3))
            def _():
                pl.semaphore_signal(r_cred.at[d], inc=1, device_id={"vp": jnp.where(d == 0, down, up)}, device_id_type=MESH)

            @pl.when(s <= chips - 3)
            def _():
                pl.semaphore_signal(q_cred.at[d], inc=1, device_id={"vp": mate}, device_id_type=MESH)

    pairs = 2 * chips

    @pl.loop(0, pairs)
    def _(j):
        d, s, chip = bwd_place(j)
        slot = lax.rem(s, 2)
        blks = (chip * 2 + core, chip * 2 + 1 - core)
        for side in (0, 1):
            blk = blks[side]
            lanes = pl.ds(side * half, half)
            lab = aux_all[blk, d, 0:1, :].astype(jnp.int32) - col_start
            mask = aux_all[blk, d, 1:2, :]
            weight = mask / mask_total
            lse = lse_all[blk, d]
            h_pair[pl.ds(side * half, half), :] = h_all[blk, d]
            z_in(side, j).wait()
            t8 = jnp.zeros((8, half), F32)
            for i in range(cols // vchunk):
                rows = pl.ds(i * vchunk, vchunk)
                z = zbuf[side, rows, :]
                hit = lax.broadcasted_iota(jnp.int32, (vchunk, half), 0) + i * vchunk == lab
                prob = jnp.exp(z - lse)
                dzb[rows, lanes] = (jnp.where(hit, prob - 1.0, prob) * weight).astype(BF16)
                t8 = t8 + jnp.sum(jnp.where(hit, z, 0.0).reshape(vchunk // 8, 8, half), axis=0)
            t_acc[...] += t8 * mask

            @pl.when(j + 1 < pairs)
            def _():
                z_in(side, j + 1).start()

        @pl.when(s >= 2)
        def _():
            mate_sum(d, slot).wait_send()
            for sb in (0, 1):
                ring_sum(d, slot, sb).wait_send()

        def partial(side, dst):
            g = jnp.dot(w_v[...], dzb[:, pl.ds(side * half, half)], preferred_element_type=F32)
            for sb in (0, 1):
                dst[d, slot, sb] = g[:, sb * sub:(sb + 1) * sub]

        partial(1, give)

        @pl.when(s >= 2)
        def _():
            pl.semaphore_wait(q_cred.at[d], 1)
        mate_sum(d, slot).start()
        partial(0, own)

        @pl.loop(0, cols // vchunk)
        def _(i):
            r0 = pl.multiple_of(i * vchunk, vchunk)
            rows = pl.ds(r0, vchunk)
            dw_acc[rows, :] += jnp.dot(dzb[rows, :], h_pair[...], preferred_element_type=F32)

        event(j, 0)

        @pl.when(j >= 1)
        def _():
            event(j - 1, 1)

    dw_copy = pltpu.make_async_copy(dw_acc, dwt_hbm, dw_sem)
    dw_copy.start()
    event(pairs - 1, 1)

    last_slot = (chips - 1) % 2
    dg = jnp.zeros((1, depth), F32)
    dc = jnp.zeros((1, depth), F32)
    for hf in (0, 1):
        for sb in (0, 1):
            rows = pl.ds(hf * half + sb * sub, sub)
            dh = own[hf, last_slot, sb].T
            normed, inv_std = normed_rows(x_ref[rows, :])
            dg = dg + jnp.sum(dh * normed, axis=0, keepdims=True)
            dc = dc + jnp.sum(dh, axis=0, keepdims=True)
            scaled = dh * gain
            mean_q = jnp.mean(scaled, axis=-1, keepdims=True)
            mean_qn = jnp.mean(scaled * normed, axis=-1, keepdims=True)
            dx_ref[rows, :] = (inv_std * (scaled - mean_q - normed * mean_qn)).astype(BF16)
    fin_all[me, 0:1, :] = dg
    fin_all[me, 1:2, :] = dc
    t_here = jnp.sum(jnp.sum(t_acc[...], axis=0, keepdims=True), axis=1, keepdims=True)
    fin_all[me, 2:3, :] = jnp.broadcast_to(t_here, (1, depth))
    fin_all[me, 3:4, :] = jnp.zeros((1, depth), F32)
    spread(fin_all.at[me], fin_all.at[me], e_send, e_recv)
    lse_sum = functools.reduce(
        jnp.add, [aux_all[i, hf, 1:2, :] * lse_all[i, hf] for i in range(n) for hf in (0, 1)])
    lse_total = jnp.sum(lse_sum, axis=1, keepdims=True)
    collect(fin_all, e_send, e_recv)
    dgain_ref[...] = functools.reduce(jnp.add, [fin_all[i, 0:1, :] for i in range(n)])
    dbias_ref[...] = functools.reduce(jnp.add, [fin_all[i, 1:2, :] for i in range(n)])
    t_total = functools.reduce(jnp.add, [fin_all[i, 2:3, 0:128] for i in range(n)])
    loss_ref[...] = (lse_total - t_total) / mask_total

    for k in range(1, chips):
        for d in (0, 1):
            ring_copy(d, k, me, 0).wait_send()
    for k in range(chips):
        for d in (0, 1):
            mate_copy(d, k, me, 0).wait_send()
    drain(aux_all.at[me], a_send, a_recv)
    drain(st_loc.at[me], s_send, s_recv)
    drain(lse_all.at[me], l_send, l_recv)
    drain(fin_all.at[me], e_send, e_recv)
    for d in (0, 1):
        for sb in (0, 1):
            ring_sum(d, (chips - 2) % 2, sb).wait_send()
        for slot in (0, 1):
            mate_sum(d, slot).wait_send()
    dw_copy.wait()


def head_call(n, x, gain, bias, w, aux):
    tokens, depth = x.shape
    cols = w.shape[1]
    half = tokens // 2
    sub = half // 2
    chips = n // 2
    vmem = pl.BlockSpec(memory_space=pltpu.VMEM)
    anywhere = pl.BlockSpec(memory_space=pl.ANY)
    dma = pltpu.SemaphoreType.DMA
    return pl.pallas_call(
        functools.partial(head_kernel, n),
        out_shape=(
            jax.ShapeDtypeStruct((tokens, depth), BF16),
            jax.ShapeDtypeStruct((cols, depth), F32),
            jax.ShapeDtypeStruct((1, depth), F32),
            jax.ShapeDtypeStruct((1, depth), F32),
            jax.ShapeDtypeStruct((1, 128), F32),
            jax.ShapeDtypeStruct((2 * n, cols, half), F32),
        ),
        in_specs=[vmem, vmem, vmem, anywhere, vmem],
        out_specs=(vmem, anywhere, vmem, vmem, vmem, anywhere),
        scratch_shapes=[
            pltpu.VMEM((depth, cols), BF16),
            pltpu.VMEM((cols, depth), BF16),
            pltpu.VMEM((n, 2, half, depth), BF16),
            pltpu.VMEM((cols, depth), F32),
            pltpu.VMEM((2, cols, half), F32),
            pltpu.VMEM((cols, tokens), BF16),
            pltpu.VMEM((tokens, depth), BF16),
            pltpu.VMEM((2, 2, 2, depth, sub), F32),
            pltpu.VMEM((2, 2, 2, depth, sub), F32),
            pltpu.VMEM((2, 2, 2, depth, sub), F32),
            pltpu.VMEM((2, 2, 2, depth, sub), F32),
            pltpu.VMEM((n, 2, 2, half), F32),
            pltpu.VMEM((n, 2, 2, half), F32),
            pltpu.VMEM((n, 2, 2, half), F32),
            pltpu.VMEM((n, 2, 1, half), F32),
            pltpu.VMEM((8, half), F32),
            pltpu.VMEM((n, 4, depth), F32),
            dma, dma, dma((2,)),
            dma((2, chips)), dma((2, chips)), dma((2, chips)), dma((2, chips)),
            dma((n,)), dma((n,)), dma((n,)), dma((n,)), dma((n,)), dma((n,)), dma((n,)), dma((n,)),
            dma((2, 2, 2)), dma((2, 2, 2)), dma((2, 2)), dma((2, 2)),
            pltpu.SemaphoreType.REGULAR((2,)), pltpu.SemaphoreType.REGULAR((2,)),
        ],
        compiler_params=pltpu.CompilerParams(
            collective_id=0, has_side_effects=True, vmem_limit_bytes=67000000),
        name="head",
    )(x, gain, bias, w, aux)


def solution(mesh):
    n = mesh.shape["vp"]

    def per_device(hidden, norm_gain, norm_bias, w_blk, labels, loss_mask):
        seq, batch, depth = hidden.shape
        tokens = seq * batch
        aux = jnp.stack(
            [labels.astype(F32).reshape(2, tokens // 2), loss_mask.reshape(2, tokens // 2)], axis=1)
        dx, dwt, dgain, dbias, loss, _ = head_call(
            n, hidden.reshape(tokens, depth), norm_gain.reshape(1, depth), norm_bias.reshape(1, depth), w_blk, aux)
        return loss[0, :1], dx.reshape(seq, batch, depth), dwt.T, dgain[0], dbias[0]

    tok_spec = P("vp", "dp")
    return jax.shard_map(
        per_device,
        mesh=mesh,
        in_specs=(P("vp", "dp", None), P(None), P(None), P(None, "vp"), tok_spec, tok_spec),
        out_specs=(P("dp"), P("vp", "dp", None), P("dp", "vp"), P("dp"), P("dp")),
        check_vma=False,
    )
```

time: 575 us -> 308 us (0.54)
  Pallas kernels: 0 us -> 287 us
  blocking collectives: 173 us -> 0 us
  matrix products: 156 us -> 0 us
  waiting for transfers between devices: 128 us -> 0 us
  other arithmetic: 97.2 us -> 3.86 us
  between operations: 16.7 us -> 1.82 us
  local copies, waits for them, and re-layouts: 1.88 us -> 14.8 us
    pallas_call x0 -> x1, Pallas kernels: none -> 287 us  [head_call(): pl.pallas_call(functools.partial(head_kernel, n), out_shape=(jax.ShapeDty...]
    dot_general x3 -> x0, matrix products: 156 us -> none  [the longest x1 55 us: per_device(): jnp.einsum('sbd,dv->sbv', h_all, w_blk, preferred_element_type=jnp.float32)]
    psum x2 -> x0, blocking collectives: 90.1 us -> none  [the longest x1 45.9 us: per_device(): sum_exp = lax.psum(jnp.sum(exp_shift, axis=-1), 'vp')]
    reduce_scatter x1 -> x0, waiting for transfers between devices: 89.8 us -> none  [per_device(): lax.psum_scatter(grad_h_part, 'vp', scatter_dimension=0, tiled=True)]
    convert_element_type x3 -> x1, other arithmetic: 55.6 us -> 0.7 us  [per_device(): labels.astype(F32).reshape(2, tokens // 2)]
    pmax x1 -> x0, blocking collectives: 43.6 us -> none  [per_device(): row_max = lax.pmax(jnp.max(logits, axis=-1), 'vp')]
    reduce_sum x6 -> x0, other arithmetic: 40.1 us -> none  [the longest x1 33.1 us: per_device(): sum_exp = lax.psum(jnp.sum(exp_shift, axis=-1), 'vp')]
    all_gather x2 -> x0, blocking collectives: 39 us -> none  [the longest x1 23.4 us: per_device(): mask_all = lax.all_gather(loss_mask, 'vp', axis=0, tiled=True)]
  transfers between devices with their start and end apart: 2 -> 0, of which waited for: 2 -> 0; matrix products, arithmetic and copies ran while one was open for 9% -> 0% of each run, Pallas kernels for 0% -> 0%
where the time goes in v1:
time: 308 us; the launch traced here: 307 us
  Pallas kernels  287 us (93%)
  local copies, waits for them, and re-layouts  14.8 us (5%)
  other arithmetic  3.86 us (1%)
    pallas_call x1, Pallas kernels, head_call(): pl.pallas_call(functools.partial(head_kernel, n), out_shape=(jax.ShapeDty...  287 us
    unnamed x6, local copies, waits for them, and re-layouts  11.4 us

profile of v1, /device:TPU:21, one launch (start us, length us, event | category | flops | bytes accessed | tf_op | source)
XLA Modules:
  0.0 307.1 jit_solution(897145416462494431)
XLA Ops:
  0.6 0.8 stack_reshape.7
  1.4 1.3 reshape.23.gain_ref
  2.7 1.3 reshape.24.bias_ref
  3.9 0.7 convert_element_type.3
  4.6 0.1 stack_reshape.6
  4.7 0.6 pad_maximum_fusion.aux_ref
  5.3 286.6 %head.1 = (bf16[512,768]{1,0:T(8,128)(2,1)}, f32[3200,768]{1,0:T(8,128)}, f32[1,768]{1,0:T(1,128)}, f32[1,768]{1,0:T(1,128)}, f32[1,128]{1,0:T(1,128)}, /*index=5*/f32[32,3200,256]{2,1,0:T(8,128)}) custom-call(bf16[512,768]{1,0:T(8,128)(2,1)} %bitcast.7, f32[1,768]{1,0:T(1,128)} %reshape.23.gain_ref, f32[1,768]{1,0:T(1,128)} %reshape.24.bias_ref, ...), custom_call_target="tpu_custom_call" | custom-call | tf_op jit(solution)/shard_map/head/pallas_call | solution.py:379
  292.0 1.3 reduce
  293.3 1.3 reduce.1
  294.5 0.0 copy-start.1
  294.5 0.0 copy-start
  294.5 10.5 %copy.11 = f32[768,3200]{1,0:T(8,128)} copy(f32[768,3200]{0,1:T(8,128)} %bitcast.5) | data formatting | bytes 19660800
  305.0 0.0 copy-done.1
  305.1 0.0 copy-done
  305.1 0.9 copy.15
Async XLA Ops:
  294.5 10.5 %copy-start.1 = (f32[1,128]{1,0:T(1,128)S(1)}, f32[1,128]{1,0:T(1,128)}, u32[]{:S(2)}) copy-start(f32[1,128]{1,0:T(1,128)} %get-tuple-element.10) | copy-start | bytes 1540
  294.5 10.6 %copy-start = (bf16[512,768]{1,0:T(8,128)(2,1)S(1)}, bf16[512,768]{1,0:T(8,128)(2,1)}, u32[]{:S(2)}) copy-start(bf16[512,768]{1,0:T(8,128)(2,1)} %get-tuple-element.11) | copy-start | bytes 2359300

commit v2 on v1

v2 whole, which is shorter than its diff:
```python
import functools

import jax
import jax.numpy as jnp
from jax import lax
from jax.experimental import pallas as pl
from jax.experimental.pallas import tpu as pltpu
from jax.sharding import PartitionSpec as P

NORM_EPS = 1e-5
F32 = jnp.float32
BF16 = jnp.bfloat16
MESH = pl.DeviceIdType.MESH


def row_chunk(rows, limit):
    best = 16
    for size in range(16, limit + 1, 16):
        if rows % size == 0:
            best = size
    return best


def head_kernel(
    n, x_hbm, affine_ref, w_hbm, aux_ref,
    dx_hbm, dwt_hbm, dgain_ref, dbias_ref, loss_ref, z_hbm,
    w_v, wt, h_all, dw_acc, z_even, z_odd, dzb, h_pair, own, give, ring_in, mate_in,
    aux_all, st_loc, st_all, lse_all, t_acc, fin_all,
    w_sem, dw_sem, x_sem, dx_sem, z_sem,
    f_send, f_recv, p_send, p_recv,
    a_send, a_recv, s_send, s_recv, l_send, l_recv, e_send, e_recv,
    r_send, r_recv, q_send, q_recv, r_cred, q_cred,
):
    chips = n // 2
    me = lax.axis_index("vp")
    zc, core = me // 2, me % 2
    mate = zc * 2 + 1 - core
    up = lax.rem(zc + 1, chips) * 2 + core
    down = lax.rem(zc + chips - 1, chips) * 2 + core
    ahead = (up, down)
    depth, cols = w_v.shape
    half = x_hbm.shape[1]
    tokens = 2 * half
    sub = half // 2
    vchunk = row_chunk(cols, 640)
    col_start = me * cols

    def remote(src, dst, send, recv, dev):
        return pltpu.make_async_remote_copy(
            src_ref=src, dst_ref=dst, send_sem=send, recv_sem=recv,
            device_id={"vp": dev}, device_id_type=MESH)

    def peer_of(k):
        return lax.rem(me + k, n)

    x_first = [pltpu.make_async_copy(x_hbm.at[hf], h_pair.at[pl.ds(hf * half, half)], x_sem.at[hf]) for hf in (0, 1)]
    for copy in x_first:
        copy.start()
    w_copy = pltpu.make_async_copy(w_hbm, w_v, w_sem)
    w_copy.start()

    barrier = pltpu.get_barrier_semaphore()
    for k in range(1, n):
        pl.semaphore_signal(barrier, inc=1, device_id={"vp": peer_of(k)}, device_id_type=MESH)

    gain = 1.0 + affine_ref[0:1, :]
    bias = affine_ref[1:2, :]

    def normed_rows(rows):
        xf = rows.astype(F32)
        centered = xf - jnp.mean(xf, axis=-1, keepdims=True)
        inv_std = lax.rsqrt(jnp.mean(centered * centered, axis=-1, keepdims=True) + NORM_EPS)
        return centered * inv_std, inv_std

    ln_rows = half // 4
    for copy in x_first:
        copy.wait()

    @pl.loop(0, 8)
    def _(i):
        row0 = pl.multiple_of((i % 4) * ln_rows, ln_rows)
        src0 = pl.multiple_of(i * ln_rows, ln_rows)
        normed, _ = normed_rows(h_pair[pl.ds(src0, ln_rows), :])
        h_all[me, i // 4, pl.ds(row0, ln_rows), :] = (normed * gain + bias).astype(BF16)

    aux_all[me] = aux_ref[...]
    t_acc[...] = jnp.zeros_like(t_acc)
    pl.semaphore_wait(barrier, n - 1)

    def ring_copy(d, k, blk, hf):
        ref = h_all.at[blk, hf]
        return remote(ref, ref, f_send.at[d, k], f_recv.at[d, k], ahead[d])

    def mate_copy(d, k, blk, hf):
        ref = h_all.at[blk, hf]
        return remote(ref, ref, p_send.at[d, k], p_recv.at[d, k], mate)

    def fwd_half(d, k):
        return (k + 1) % 2 if d == 0 else k % 2

    for k in (1, 2):
        for d in (0, 1):
            ring_copy(d, k, me, fwd_half(d, k)).start()

    def spread(ref, dst, send, recv):
        for k in range(1, n):
            remote(ref, dst, send.at[k], recv.at[me], peer_of(k)).start()

    def collect(ref_all, send, recv):
        for k in range(1, n):
            src = peer_of(k)
            remote(ref_all.at[src], ref_all.at[src], send.at[k], recv.at[src], src).wait_recv()

    def drain(ref, send, recv):
        for k in range(1, n):
            remote(ref, ref, send.at[k], recv.at[me], peer_of(k)).wait_send()

    spread(aux_all.at[me], aux_all.at[me], a_send, a_recv)

    w_copy.wait()
    tcols = 128 if cols % 128 == 0 else cols

    @pl.loop(0, cols // tcols)
    def _(i):
        c0 = pl.multiple_of(i * tcols, tcols)
        wt[pl.ds(c0, tcols), :] = w_v[:, pl.ds(c0, tcols)].T

    last = chips - 1

    z_stage = (z_even, z_odd)
    dz_refs = (dzb, wt.at[:, pl.ds(0, tokens)])

    def z_out(side, d, tile):
        src = z_stage[side].at[:, pl.ds(d * half, half)]
        return pltpu.make_async_copy(src, z_hbm.at[tile], z_sem.at[side, d])

    def fwd_chip(d, k):
        step = (k + 1) // 2
        return lax.rem(zc + chips - step, chips) if d == 0 else lax.rem(zc + step, chips)

    @pl.loop(0, chips)
    def _(k):
        for d in (0, 1):
            blk = fwd_chip(d, k) * 2 + core
            hf = fwd_half(d, k)

            @pl.when(k >= 1)
            def _():
                ring_copy(d, k, blk, hf).wait_recv()

                @pl.when(k + 2 <= last)
                def _():
                    ring_copy(d, k + 2, blk, hf).start()

            mate_copy(d, k, blk, hf).start()

        for side in (0, 1):
            places = [(fwd_chip(d, k) * 2 + (core if side == 0 else 1 - core), fwd_half(d, k)) for d in (0, 1)]
            for d in (0, 1):
                if side == 1:
                    mate_copy(d, k, *places[d]).wait_recv()
                h_pair[pl.ds(d * half, half), :] = h_all[places[d]]

            @pl.when(k >= 1)
            def _():
                for d in (0, 1):
                    z_out(side, d, 0).wait()

            m8 = jnp.full((8, tokens), -jnp.inf, F32)
            s8 = jnp.zeros((8, tokens), F32)
            h_tile = h_pair[...]
            for j in range(cols // vchunk):
                rows = pl.ds(j * vchunk, vchunk)
                z = lax.dot_general(wt[rows, :], h_tile, (((1,), (1,)), ((), ())), preferred_element_type=F32)
                z_stage[side][rows, 0:tokens] = z
                z3 = z.reshape(vchunk // 8, 8, tokens)
                m_new = jnp.maximum(m8, jnp.max(z3, axis=0))
                s8 = s8 * jnp.exp(m8 - m_new) + jnp.sum(jnp.exp(z3 - m_new[None]), axis=0)
                m8 = m_new
            m1 = jnp.max(m8, axis=0, keepdims=True)
            s1 = jnp.sum(s8 * jnp.exp(m8 - m1), axis=0, keepdims=True)
            for d in (0, 1):
                blk, hf = places[d]
                lanes = slice(d * half, (d + 1) * half)
                st_loc[blk, hf, 0:1, :] = m1[:, lanes]
                st_loc[blk, hf, 1:2, :] = s1[:, lanes]
                z_out(side, d, blk * 2 + hf).start()

    def bwd_chip(d, s):
        return lax.rem(zc + 2 * chips + (2 * d - 1) * (s + 1), chips)

    def z_in(side, d, s):
        blk = bwd_chip(d, s) * 2 + (core if side == 0 else 1 - core)
        return pltpu.make_async_copy(z_hbm.at[blk * 2 + d], z_stage[d].at[:, pl.ds(side * half, half)], z_sem.at[d, side])

    for k in range(1, n):
        peer = peer_of(k)
        remote(st_loc.at[peer], st_all.at[me], s_send.at[k], s_recv.at[me], peer).start()
    st_all[me] = st_loc[me]
    for side in (0, 1):
        for d in (0, 1):
            z_out(side, d, 0).wait()
    for d in (0, 1):
        for side in (0, 1):
            z_in(side, d, 0).start()

    @pl.loop(0, cols // vchunk)
    def _(i):
        c0 = pl.multiple_of(i * vchunk, vchunk)
        dw_acc[pl.ds(c0, vchunk), :] = jnp.zeros((vchunk, depth), F32)

    collect(st_all, s_send, s_recv)
    for hf in (0, 1):
        tops = [st_all[i, hf, 0:1, :] for i in range(n)]
        top = functools.reduce(jnp.maximum, tops)
        total = functools.reduce(jnp.add, [st_all[i, hf, 1:2, :] * jnp.exp(tops[i] - top) for i in range(n)])
        lse_all[me, hf] = top + jnp.log(total)
    spread(lse_all.at[me], lse_all.at[me], l_send, l_recv)
    collect(aux_all, a_send, a_recv)
    mask_sum = functools.reduce(jnp.add, [aux_all[i, hf, 1:2, :] for i in range(n) for hf in (0, 1)])
    mask_total = jnp.sum(mask_sum, axis=1, keepdims=True)
    collect(lse_all, l_send, l_recv)
    for k in range(1, chips):
        for d in (0, 1):
            ring_copy(d, k, me, 0).wait_send()
    for k in range(chips):
        for d in (0, 1):
            mate_copy(d, k, me, 0).wait_send()

    def ring_sum(d, slot, sb):
        return remote(own.at[d, slot, sb], ring_in.at[d, slot, sb], r_send.at[d, slot, sb], r_recv.at[d, slot, sb],
                      ahead[d])

    def mate_sum(d, slot):
        return remote(give.at[d], mate_in.at[d, slot], q_send.at[d], q_recv.at[d, slot], mate)

    def event(d, s, sb):
        slot = lax.rem(s, 2)
        prev = lax.rem(s + 1, 2)
        if sb == 0:
            mate_sum(d, slot).wait_recv()

        @pl.when(s == 0)
        def _():
            own[d, slot, sb] = own[d, slot, sb] + mate_in[d, slot, sb]

        @pl.when(s >= 1)
        def _():
            ring_sum(d, prev, sb).wait_recv()
            own[d, slot, sb] = (own[d, slot, sb] + mate_in[d, slot, sb]) + ring_in[d, prev, sb]

        @pl.when(s <= chips - 2)
        def _():
            if sb == 0:
                @pl.when(s >= 2)
                def _():
                    pl.semaphore_wait(r_cred.at[d], 1)
            ring_sum(d, slot, sb).start()

        if sb == 1:
            @pl.when((s >= 1) & (s <= chips - 3))
            def _():
                pl.semaphore_signal(r_cred.at[d], inc=1, device_id={"vp": ahead[1 - d]}, device_id_type=MESH)

            @pl.when(s <= chips - 3)
            def _():
                pl.semaphore_signal(q_cred.at[d], inc=1, device_id={"vp": mate}, device_id_type=MESH)

    kchunk = 768 if cols > 768 else cols

    def dz_rows(d, blk, lanes, r0, size):
        lab = aux_all[blk, d, 0:1, :].astype(jnp.int32) - (col_start + r0)
        weight = aux_all[blk, d, 1:2, :] / mask_total
        z = z_stage[d][pl.ds(r0, size), lanes]
        hit = lax.broadcasted_iota(jnp.int32, (size, half), 0) == lab
        prob = jnp.exp(z - lse_all[blk, d])
        dz_refs[d][pl.ds(r0, size), lanes] = (jnp.where(hit, prob - 1.0, prob) * weight).astype(BF16)
        return jnp.sum(jnp.where(hit, z, 0.0).reshape(size // 8, 8, half), axis=0)

    @pl.loop(0, chips)
    def _(s):
        slot = lax.rem(s, 2)
        for d in (0, 1):
            for side in (0, 1):
                z_in(side, d, s).wait()

            @pl.when(s >= 1)
            def _():
                mate_sum(d, slot).wait_send()

            @pl.when(s >= 2)
            def _():
                for sb in (0, 1):
                    ring_sum(d, slot, sb).wait_send()

            blks = [bwd_chip(d, s) * 2 + (core if side == 0 else 1 - core) for side in (0, 1)]
            t8 = [jnp.zeros((8, half), F32), jnp.zeros((8, half), F32)]
            g = jnp.zeros((depth, tokens), F32)
            for r0 in range(0, cols, kchunk):
                size = min(kchunk, cols - r0)
                for side in (0, 1):
                    t8[side] = t8[side] + dz_rows(d, blks[side], slice(side * half, (side + 1) * half), r0, size)
                g = g + jnp.dot(w_v[:, r0:r0 + size], dz_refs[d][r0:r0 + size, :], preferred_element_type=F32)
            for side in (0, 1):
                t_acc[...] += t8[side] * aux_all[blks[side], d, 1:2, :]
            for sb in (0, 1):
                own[d, slot, sb] = g[:, sb * sub:(sb + 1) * sub]
                give[d, sb] = g[:, half + sb * sub:half + (sb + 1) * sub]

            @pl.when(s + 1 < chips)
            def _():
                for side in (0, 1):
                    z_in(side, d, s + 1).start()

            @pl.when(s >= 2)
            def _():
                pl.semaphore_wait(q_cred.at[d], 1)
            mate_sum(d, slot).start()

        for d in (0, 1):
            event(d, s, 0)

        for d in (0, 1):
            chip = bwd_chip(d, s)
            h_pair[0:half, :] = h_all[chip * 2 + core, d]
            h_pair[half:tokens, :] = h_all[chip * 2 + 1 - core, d]
            h_tile = h_pair[...]
            for i in range(cols // vchunk):
                rows = pl.ds(i * vchunk, vchunk)
                dw_acc[rows, :] += jnp.dot(dz_refs[d][rows, :], h_tile, preferred_element_type=F32)

        @pl.when(s < chips - 1)
        def _():
            for d in (0, 1):
                event(d, s, 1)

    dw_copy = pltpu.make_async_copy(dw_acc, dwt_hbm, dw_sem)
    dw_copy.start()
    x_again = pltpu.make_async_copy(x_hbm, h_all.at[0], x_sem.at[0])
    x_again.start()
    for d in (0, 1):
        event(d, chips - 1, 1)

    x_again.wait()
    last_slot = (chips - 1) % 2
    dg = jnp.zeros((1, depth), F32)
    dc = jnp.zeros((1, depth), F32)
    for hf in (0, 1):
        for sb in (0, 1):
            rows = slice(sb * sub, (sb + 1) * sub)
            dh = own[hf, last_slot, sb].T
            normed, inv_std = normed_rows(h_all[0, hf, rows, :])
            dg = dg + jnp.sum(dh * normed, axis=0, keepdims=True)
            dc = dc + jnp.sum(dh, axis=0, keepdims=True)
            scaled = dh * gain
            mean_q = jnp.mean(scaled, axis=-1, keepdims=True)
            mean_qn = jnp.mean(scaled * normed, axis=-1, keepdims=True)
            h_all[1, hf, rows, :] = (inv_std * (scaled - mean_q - normed * mean_qn)).astype(BF16)
    dx_copy = pltpu.make_async_copy(h_all.at[1], dx_hbm, dx_sem)
    dx_copy.start()
    fin_all[me, 0:1, :] = dg
    fin_all[me, 1:2, :] = dc
    t_here = jnp.sum(jnp.sum(t_acc[...], axis=0, keepdims=True), axis=1, keepdims=True)
    fin_all[me, 2:3, :] = jnp.broadcast_to(t_here, (1, depth))
    fin_all[me, 3:4, :] = jnp.zeros((1, depth), F32)
    spread(fin_all.at[me], fin_all.at[me], e_send, e_recv)
    lse_sum = functools.reduce(
        jnp.add, [aux_all[i, hf, 1:2, :] * lse_all[i, hf] for i in range(n) for hf in (0, 1)])
    lse_total = jnp.sum(lse_sum, axis=1, keepdims=True)
    collect(fin_all, e_send, e_recv)
    dgain_ref[...] = functools.reduce(jnp.add, [fin_all[i, 0:1, :] for i in range(n)])
    dbias_ref[...] = functools.reduce(jnp.add, [fin_all[i, 1:2, :] for i in range(n)])
    t_total = functools.reduce(jnp.add, [fin_all[i, 2:3, 0:128] for i in range(n)])
    loss_ref[...] = (lse_total - t_total) / mask_total

    drain(aux_all.at[me], a_send, a_recv)
    drain(st_loc.at[me], s_send, s_recv)
    drain(lse_all.at[me], l_send, l_recv)
    drain(fin_all.at[me], e_send, e_recv)
    for d in (0, 1):
        for sb in (0, 1):
            ring_sum(d, (chips - 2) % 2, sb).wait_send()
        mate_sum(d, 0).wait_send()
    dw_copy.wait()
    dx_copy.wait()


def head_call(n, x, affine, w, aux):
    _, half, depth = x.shape
    tokens = 2 * half
    cols = w.shape[1]
    sub = half // 2
    chips = n // 2
    vmem = pl.BlockSpec(memory_space=pltpu.VMEM)
    anywhere = pl.BlockSpec(memory_space=pl.ANY)
    dma = pltpu.SemaphoreType.DMA
    return pl.pallas_call(
        functools.partial(head_kernel, n),
        out_shape=(
            jax.ShapeDtypeStruct((2, half, depth), BF16),
            jax.ShapeDtypeStruct((cols, depth), F32),
            jax.ShapeDtypeStruct((1, depth), F32),
            jax.ShapeDtypeStruct((1, depth), F32),
            jax.ShapeDtypeStruct((1, 128), F32),
            jax.ShapeDtypeStruct((2 * n, cols, half), F32),
        ),
        in_specs=[anywhere, vmem, anywhere, vmem],
        out_specs=(anywhere, anywhere, vmem, vmem, vmem, anywhere),
        scratch_shapes=[
            pltpu.VMEM((depth, cols), BF16),
            pltpu.VMEM((cols, depth), BF16),
            pltpu.VMEM((n, 2, half, depth), BF16),
            pltpu.VMEM((cols, depth), F32),
            pltpu.VMEM((cols, tokens), F32),
            pltpu.VMEM((cols, tokens), F32),
            pltpu.VMEM((cols, tokens), BF16),
            pltpu.VMEM((tokens, depth), BF16),
            pltpu.VMEM((2, 2, 2, depth, sub), F32),
            pltpu.VMEM((2, 2, depth, sub), F32),
            pltpu.VMEM((2, 2, 2, depth, sub), F32),
            pltpu.VMEM((2, 2, 2, depth, sub), F32),
            pltpu.VMEM((n, 2, 2, half), F32),
            pltpu.VMEM((n, 2, 2, half), F32),
            pltpu.VMEM((n, 2, 2, half), F32),
            pltpu.VMEM((n, 2, 1, half), F32),
            pltpu.VMEM((8, half), F32),
            pltpu.VMEM((n, 4, depth), F32),
            dma, dma, dma((2,)), dma, dma((2, 2)),
            dma((2, chips)), dma((2, chips)), dma((2, chips)), dma((2, chips)),
            dma((n,)), dma((n,)), dma((n,)), dma((n,)), dma((n,)), dma((n,)), dma((n,)), dma((n,)),
            dma((2, 2, 2)), dma((2, 2, 2)), dma((2,)), dma((2, 2)),
            pltpu.SemaphoreType.REGULAR((2,)), pltpu.SemaphoreType.REGULAR((2,)),
        ],
        compiler_params=pltpu.CompilerParams(
            collective_id=0, has_side_effects=True, vmem_limit_bytes=67000000),
        name="head",
    )(x, affine, w, aux)


def flip_kernel(x_ref, y_ref):
    y_ref[...] = x_ref[...].T


def flip(x):
    rows, depth = x.shape
    size = 640 if rows % 640 == 0 else rows
    return pl.pallas_call(
        flip_kernel,
        grid=(rows // size,),
        out_shape=jax.ShapeDtypeStruct((depth, rows), x.dtype),
        in_specs=[pl.BlockSpec((size, depth), lambda i: (i, 0))],
        out_specs=pl.BlockSpec((depth, size), lambda i: (0, i)),
        name="flip",
    )(x)


def solution(mesh):
    n = mesh.shape["vp"]

    def per_device(hidden, norm_gain, norm_bias, w_blk, labels, loss_mask):
        seq, batch, depth = hidden.shape
        tokens = seq * batch
        aux = jnp.stack(
            [labels.astype(F32).reshape(2, tokens // 2), loss_mask.reshape(2, tokens // 2)], axis=1)
        dx, dwt, dgain, dbias, loss, _ = head_call(
            n, hidden.reshape(2, tokens // 2, depth), jnp.stack([norm_gain, norm_bias]), w_blk, aux)
        return loss[0, :1], dx.reshape(seq, batch, depth), flip(dwt), dgain[0], dbias[0]

    tok_spec = P("vp", "dp")
    return jax.shard_map(
        per_device,
        mesh=mesh,
        in_specs=(P("vp", "dp", None), P(None), P(None), P(None, "vp"), tok_spec, tok_spec),
        out_specs=(P("dp"), P("vp", "dp", None), P("dp", "vp"), P("dp"), P("dp")),
        check_vma=False,
    )
```

time: 308 us -> 249 us (0.81)
  Pallas kernels: 287 us -> 240 us
  local copies, waits for them, and re-layouts: 14.8 us -> 3.12 us
    pallas_call x1, Pallas kernels: 287 us -> 229 us  [head_call(): pl.pallas_call(functools.partial(head_kernel, n), out_shape=(jax.ShapeDty...]
    pallas_call x0 -> x1, Pallas kernels: none -> 10.5 us  [flip(): pl.pallas_call(flip_kernel, grid=(rows // size,), out_shape=jax.ShapeDtyp...]
    unnamed x6 -> x5, local copies, waits for them, and re-layouts: 11.4 us -> 0.89 us
where the time goes in v2:
time: 249 us
  Pallas kernels  240 us (96%)
  other arithmetic  4.47 us (2%)
  local copies, waits for them, and re-layouts  3.12 us (1%)
    pallas_call x1, Pallas kernels, head_call(): pl.pallas_call(functools.partial(head_kernel, n), out_shape=(jax.ShapeDty...  229 us
    pallas_call x1, Pallas kernels, flip(): pl.pallas_call(flip_kernel, grid=(rows // size,), out_shape=jax.ShapeDtyp...  10.5 us

profile of v2, /device:TPU:21, one launch (start us, length us, event | category | flops | bytes accessed | tf_op | source)
XLA Modules:
  0.0 249.0 jit_solution(3919702039981089418)
XLA Ops:
  0.6 0.8 stack_reshape.7
  1.4 0.7 stack.12
  2.1 0.7 stack.13
  2.8 0.6 pad_maximum_fusion.affine_ref
  3.4 0.7 convert_element_type.3
  4.1 0.1 stack_reshape.6
  4.2 0.6 pad_maximum_fusion.1.aux_ref
  4.8 229.1 %head.1 = (bf16[2,256,768]{2,1,0:T(8,128)(2,1)}, f32[3200,768]{1,0:T(8,128)}, f32[1,768]{1,0:T(1,128)}, f32[1,768]{1,0:T(1,128)}, f32[1,128]{1,0:T(1,128)}, /*index=5*/f32[32,3200,256]{2,1,0:T(8,128)}) custom-call(bf16[2,256,768]{2,1,0:T(8,128)(2,1)} %bitcast.5, f32[2,768]{1,0:T(2,128)} %pad_maximum_fusion.affine_ref, bf16[768,3200]{1,0:T(8,128)(2,1)} %w_hbm.1, ...), custom_call_target="tpu_custom_call" | custom-call | tf_op jit(solution)/shard_map/head/pallas_call | solution.py:397
  233.9 1.3 reduce
  235.1 1.3 reduce.1
  236.4 0.0 copy-start.1
  236.4 0.0 copy-start
  236.4 10.5 %flip.1 = f32[768,3200]{1,0:T(8,128)} custom-call(f32[3200,768]{1,0:T(8,128)} %get-tuple-element.12.x_ref), custom_call_target="tpu_custom_call" | custom-call | tf_op jit(solution)/shard_map/flip/pallas_call | solution.py:447
  247.0 0.0 copy-done.1
  247.0 0.0 copy-done
  247.0 0.9 copy.14
Async XLA Ops:
  236.4 10.6 %copy-start.1 = (f32[1,128]{1,0:T(1,128)S(1)}, f32[1,128]{1,0:T(1,128)}, u32[]{:S(2)}) copy-start(f32[1,128]{1,0:T(1,128)} %get-tuple-element.10) | copy-start | bytes 1540
  236.4 10.6 %copy-start = (bf16[2,256,768]{2,1,0:T(8,128)(2,1)S(1)}, bf16[2,256,768]{2,1,0:T(8,128)(2,1)}, u32[]{:S(2)}) copy-start(bf16[2,256,768]{2,1,0:T(8,128)(2,1)} %get-tuple-element.11) | copy-start | bytes 2359300

commit v3 on v2

--- a/solution.py
+++ b/solution.py
@@ -22,13 +22,13 @@
 
 
 def head_kernel(
-    n, x_hbm, affine_ref, w_hbm, aux_ref,
-    dx_hbm, dwt_hbm, dgain_ref, dbias_ref, loss_ref, z_hbm,
+    n, x_hbm, gain_ref, bias_ref, w_hbm, aux_ref,
+    dx_hbm, dw_hbm, dgain_ref, dbias_ref, loss_ref, z_hbm,
     w_v, wt, h_all, dw_acc, z_even, z_odd, dzb, h_pair, own, give, ring_in, mate_in,
-    aux_all, st_loc, st_all, lse_all, t_acc, fin_all,
+    aux_all, st_loc, st_all, part_all, far_all, lse_all, t_acc, fin_all,
     w_sem, dw_sem, x_sem, dx_sem, z_sem,
     f_send, f_recv, p_send, p_recv,
-    a_send, a_recv, s_send, s_recv, l_send, l_recv, e_send, e_recv,
+    a_send, a_recv, s_send, s_recv, c_send, c_recv, l_send, l_recv, e_send, e_recv,
     r_send, r_recv, q_send, q_recv, r_cred, q_cred,
 ):
     chips = n // 2
@@ -63,8 +63,8 @@
     for k in range(1, n):
         pl.semaphore_signal(barrier, inc=1, device_id={"vp": peer_of(k)}, device_id_type=MESH)
 
-    gain = 1.0 + affine_ref[0:1, :]
-    bias = affine_ref[1:2, :]
+    gain = 1.0 + gain_ref[...].reshape(1, depth)
+    bias = bias_ref[...].reshape(1, depth)
 
     def normed_rows(rows):
         xf = rows.astype(F32)
@@ -126,6 +126,28 @@
         wt[pl.ds(c0, tcols), :] = w_v[:, pl.ds(c0, tcols)].T
 
     last = chips - 1
+    far = lax.rem(zc + chips // 2, chips)
+    near = [(dc * 2 + cc, lax.rem(zc + dc, chips) * 2 + (core if cc == 0 else 1 - core))
+            for dc in range(chips) for cc in (0, 1) if dc != chips // 2 and (dc, cc) != (0, 0)]
+
+    def near_copy(i, dev):
+        return remote(st_loc.at[dev], st_all.at[me], s_send.at[i], s_recv.at[me], dev)
+
+    def join(pairs):
+        top = functools.reduce(jnp.maximum, [m for m, _ in pairs])
+        return top, functools.reduce(jnp.add, [t * jnp.exp(m - top) for m, t in pairs])
+
+    def stat(ref, *at):
+        return ref[(*at, slice(0, 1))], ref[(*at, slice(1, 2))]
+
+    def join_near():
+        for _, dev in near:
+            remote(st_all.at[dev], st_all.at[dev], s_send.at[0], s_recv.at[dev], dev).wait_recv()
+        for hf in (0, 1):
+            top, total = join([stat(st_loc, me, hf)] + [stat(st_all, dev, hf) for _, dev in near])
+            part_all[me, hf, 0:1, :] = top
+            part_all[me, hf, 1:2, :] = total
+        spread(part_all.at[me], part_all.at[me], l_send, l_recv)
 
     z_stage = (z_even, z_odd)
     dz_refs = (dzb, wt.at[:, pl.ds(0, tokens)])
@@ -186,6 +208,14 @@
                 st_loc[blk, hf, 1:2, :] = s1[:, lanes]
                 z_out(side, d, blk * 2 + hf).start()
 
+            if side == 0:
+                pl.when(k == last)(join_near)
+
+        @pl.when(k == last - 1)
+        def _():
+            for i, dev in near:
+                near_copy(i, dev).start()
+
     def bwd_chip(d, s):
         return lax.rem(zc + 2 * chips + (2 * d - 1) * (s + 1), chips)
 
@@ -193,10 +223,9 @@
         blk = bwd_chip(d, s) * 2 + (core if side == 0 else 1 - core)
         return pltpu.make_async_copy(z_hbm.at[blk * 2 + d], z_stage[d].at[:, pl.ds(side * half, half)], z_sem.at[d, side])
 
-    for k in range(1, n):
-        peer = peer_of(k)
-        remote(st_loc.at[peer], st_all.at[me], s_send.at[k], s_recv.at[me], peer).start()
-    st_all[me] = st_loc[me]
+    far_part = st_loc.at[pl.ds(far * 2, 2)]
+    spread(far_part, far_all.at[me], c_send, c_recv)
+    far_all[me] = far_part[...]
     for side in (0, 1):
         for d in (0, 1):
             z_out(side, d, 0).wait()
@@ -204,22 +233,26 @@
         for side in (0, 1):
             z_in(side, d, 0).start()
 
-    @pl.loop(0, cols // vchunk)
+    zrows = row_chunk(depth, 96)
+
+    @pl.loop(0, depth // zrows)
     def _(i):
-        c0 = pl.multiple_of(i * vchunk, vchunk)
-        dw_acc[pl.ds(c0, vchunk), :] = jnp.zeros((vchunk, depth), F32)
-
-    collect(st_all, s_send, s_recv)
-    for hf in (0, 1):
-        tops = [st_all[i, hf, 0:1, :] for i in range(n)]
-        top = functools.reduce(jnp.maximum, tops)
-        total = functools.reduce(jnp.add, [st_all[i, hf, 1:2, :] * jnp.exp(tops[i] - top) for i in range(n)])
-        lse_all[me, hf] = top + jnp.log(total)
-    spread(lse_all.at[me], lse_all.at[me], l_send, l_recv)
+        r0 = pl.multiple_of(i * zrows, zrows)
+        dw_acc[pl.ds(r0, zrows), :] = jnp.zeros((zrows, cols), F32)
+
     collect(aux_all, a_send, a_recv)
     mask_sum = functools.reduce(jnp.add, [aux_all[i, hf, 1:2, :] for i in range(n) for hf in (0, 1)])
     mask_total = jnp.sum(mask_sum, axis=1, keepdims=True)
-    collect(lse_all, l_send, l_recv)
+    collect(part_all, l_send, l_recv)
+    collect(far_all, c_send, c_recv)
+
+    @pl.loop(0, n)
+    def _(b):
+        other = lax.rem(b // 2 + chips // 2, chips) * 2
+        for hf in (0, 1):
+            top, total = join([stat(part_all, b, hf)] + [stat(far_all, other + cc, lax.rem(b, 2), hf) for cc in (0, 1)])
+            lse_all[b, hf] = top + jnp.log(total)
+
     for k in range(1, chips):
         for d in (0, 1):
             ring_copy(d, k, me, 0).wait_send()
@@ -267,6 +300,8 @@
                 pl.semaphore_signal(q_cred.at[d], inc=1, device_id={"vp": mate}, device_id_type=MESH)
 
     kchunk = 768 if cols > 768 else cols
+    nchunk = 512 if cols > 512 else cols
+    ht_refs = [wt.at[pl.ds(side * depth, depth), pl.ds(tokens, half)] for side in (0, 1)]
 
     def dz_rows(d, blk, lanes, r0, size):
         lab = aux_all[blk, d, 0:1, :].astype(jnp.int32) - (col_start + r0)
@@ -321,32 +356,34 @@
             event(d, s, 0)
 
         for d in (0, 1):
-            chip = bwd_chip(d, s)
-            h_pair[0:half, :] = h_all[chip * 2 + core, d]
-            h_pair[half:tokens, :] = h_all[chip * 2 + 1 - core, d]
-            h_tile = h_pair[...]
-            for i in range(cols // vchunk):
-                rows = pl.ds(i * vchunk, vchunk)
-                dw_acc[rows, :] += jnp.dot(dz_refs[d][rows, :], h_tile, preferred_element_type=F32)
+            for side in (0, 1):
+                blk = bwd_chip(d, s) * 2 + (core if side == 0 else 1 - core)
+                ht_refs[side][...] = h_all[blk, d].T
+            for r0 in range(0, cols, nchunk):
+                size = min(nchunk, cols - r0)
+                parts = [
+                    lax.dot_general(ht_refs[side][...], dz_refs[d][r0:r0 + size, side * half:(side + 1) * half],
+                                    (((1,), (1,)), ((), ())), preferred_element_type=F32) for side in (0, 1)]
+                dw_acc[:, r0:r0 + size] += parts[0] + parts[1]
 
         @pl.when(s < chips - 1)
         def _():
             for d in (0, 1):
                 event(d, s, 1)
 
-    dw_copy = pltpu.make_async_copy(dw_acc, dwt_hbm, dw_sem)
+    dw_copy = pltpu.make_async_copy(dw_acc, dw_hbm, dw_sem)
     dw_copy.start()
     x_again = pltpu.make_async_copy(x_hbm, h_all.at[0], x_sem.at[0])
     x_again.start()
-    for d in (0, 1):
-        event(d, chips - 1, 1)
-
+    last_slot = (chips - 1) % 2
     x_again.wait()
-    last_slot = (chips - 1) % 2
     dg = jnp.zeros((1, depth), F32)
     dc = jnp.zeros((1, depth), F32)
-    for hf in (0, 1):
-        for sb in (0, 1):
+    for sb in (0, 1):
+        if sb == 1:
+            for d in (0, 1):
+                event(d, chips - 1, 1)
+        for hf in (0, 1):
             rows = slice(sb * sub, (sb + 1) * sub)
             dh = own[hf, last_slot, sb].T
             normed, inv_std = normed_rows(h_all[0, hf, rows, :])
@@ -368,14 +405,16 @@
         jnp.add, [aux_all[i, hf, 1:2, :] * lse_all[i, hf] for i in range(n) for hf in (0, 1)])
     lse_total = jnp.sum(lse_sum, axis=1, keepdims=True)
     collect(fin_all, e_send, e_recv)
-    dgain_ref[...] = functools.reduce(jnp.add, [fin_all[i, 0:1, :] for i in range(n)])
-    dbias_ref[...] = functools.reduce(jnp.add, [fin_all[i, 1:2, :] for i in range(n)])
+    dgain_ref[...] = functools.reduce(jnp.add, [fin_all[i, 0:1, :] for i in range(n)]).reshape(depth)
+    dbias_ref[...] = functools.reduce(jnp.add, [fin_all[i, 1:2, :] for i in range(n)]).reshape(depth)
     t_total = functools.reduce(jnp.add, [fin_all[i, 2:3, 0:128] for i in range(n)])
     loss_ref[...] = (lse_total - t_total) / mask_total
 
     drain(aux_all.at[me], a_send, a_recv)
-    drain(st_loc.at[me], s_send, s_recv)
-    drain(lse_all.at[me], l_send, l_recv)
+    for i, dev in near:
+        near_copy(i, dev).wait_send()
+    drain(part_all.at[me], l_send, l_recv)
+    drain(far_all.at[me], c_send, c_recv)
     drain(fin_all.at[me], e_send, e_recv)
     for d in (0, 1):
         for sb in (0, 1):
@@ -385,7 +424,7 @@
     dx_copy.wait()
 
 
-def head_call(n, x, affine, w, aux):
+def head_call(n, x, gain, bias, w, aux):
     _, half, depth = x.shape
     tokens = 2 * half
     cols = w.shape[1]
@@ -398,19 +437,19 @@
         functools.partial(head_kernel, n),
         out_shape=(
             jax.ShapeDtypeStruct((2, half, depth), BF16),
-            jax.ShapeDtypeStruct((cols, depth), F32),
-            jax.ShapeDtypeStruct((1, depth), F32),
-            jax.ShapeDtypeStruct((1, depth), F32),
+            jax.ShapeDtypeStruct((depth, cols), F32),
+            jax.ShapeDtypeStruct((depth,), F32),
+            jax.ShapeDtypeStruct((depth,), F32),
             jax.ShapeDtypeStruct((1, 128), F32),
             jax.ShapeDtypeStruct((2 * n, cols, half), F32),
         ),
-        in_specs=[anywhere, vmem, anywhere, vmem],
+        in_specs=[anywhere, vmem, vmem, anywhere, vmem],
         out_specs=(anywhere, anywhere, vmem, vmem, vmem, anywhere),
         scratch_shapes=[
             pltpu.VMEM((depth, cols), BF16),
             pltpu.VMEM((cols, depth), BF16),
             pltpu.VMEM((n, 2, half, depth), BF16),
-            pltpu.VMEM((cols, depth), F32),
+            pltpu.VMEM((depth, cols), F32),
             pltpu.VMEM((cols, tokens), F32),
             pltpu.VMEM((cols, tokens), F32),
             pltpu.VMEM((cols, tokens), BF16),
@@ -422,35 +461,38 @@
             pltpu.VMEM((n, 2, 2, half), F32),
             pltpu.VMEM((n, 2, 2, half), F32),
             pltpu.VMEM((n, 2, 2, half), F32),
+            pltpu.VMEM((n, 2, 2, half), F32),
+            pltpu.VMEM((n, 2, 2, 2, half), F32),
             pltpu.VMEM((n, 2, 1, half), F32),
             pltpu.VMEM((8, half), F32),
             pltpu.VMEM((n, 4, depth), F32),
             dma, dma, dma((2,)), dma, dma((2, 2)),
             dma((2, chips)), dma((2, chips)), dma((2, chips)), dma((2, chips)),
-            dma((n,)), dma((n,)), dma((n,)), dma((n,)), dma((n,)), dma((n,)), dma((n,)), dma((n,)),
+            dma((n,)), dma((n,)), dma((n,)), dma((n,)), dma((n,)), dma((n,)), dma((n,)), dma((n,)), dma((n,)), dma((n,)),
             dma((2, 2, 2)), dma((2, 2, 2)), dma((2,)), dma((2, 2)),
             pltpu.SemaphoreType.REGULAR((2,)), pltpu.SemaphoreType.REGULAR((2,)),
         ],
         compiler_params=pltpu.CompilerParams(
             collective_id=0, has_side_effects=True, vmem_limit_bytes=67000000),
         name="head",
-    )(x, affine, w, aux)
-
-
-def flip_kernel(x_ref, y_ref):
-    y_ref[...] = x_ref[...].T
-
-
-def flip(x):
-    rows, depth = x.shape
-    size = 640 if rows % 640 == 0 else rows
+    )(x, gain, bias, w, aux)
+
+
+def pass_kernel(x_ref, y_ref):
+    y_ref[...] = x_ref[...]
+
+
+def passed(x):
+    rows, cols = x.shape
+    size = row_chunk(rows, 128)
+    spec = pl.BlockSpec((size, cols), lambda i: (i, 0))
     return pl.pallas_call(
-        flip_kernel,
+        pass_kernel,
         grid=(rows // size,),
-        out_shape=jax.ShapeDtypeStruct((depth, rows), x.dtype),
-        in_specs=[pl.BlockSpec((size, depth), lambda i: (i, 0))],
-        out_specs=pl.BlockSpec((depth, size), lambda i: (0, i)),
-        name="flip",
+        out_shape=jax.ShapeDtypeStruct(x.shape, x.dtype),
+        in_specs=[spec],
+        out_specs=spec,
+        name="passed",
     )(x)
 
 
@@ -462,9 +504,9 @@
         tokens = seq * batch
         aux = jnp.stack(
             [labels.astype(F32).reshape(2, tokens // 2), loss_mask.reshape(2, tokens // 2)], axis=1)
-        dx, dwt, dgain, dbias, loss, _ = head_call(
-            n, hidden.reshape(2, tokens // 2, depth), jnp.stack([norm_gain, norm_bias]), w_blk, aux)
-        return loss[0, :1], dx.reshape(seq, batch, depth), flip(dwt), dgain[0], dbias[0]
+        dx, dw, dgain, dbias, loss, _ = head_call(
+            n, hidden.reshape(2, tokens // 2, depth), norm_gain, norm_bias, w_blk, aux)
+        return loss[0, :1], dx.reshape(seq, batch, depth), passed(dw), dgain, dbias
 
     tok_spec = P("vp", "dp")
     return jax.shard_map(

time: 249 us -> 242 us (0.972)
  Pallas kernels: 240 us -> 236 us
  other arithmetic: 4.47 us -> 1.3 us
    pallas_call x2 -> x0, other arithmetic: 2.56 us -> none  [head_call(): pl.pallas_call(functools.partial(head_kernel, n), out_shape=(jax.ShapeDty...]
where the time goes in v3:
time: 242 us
  Pallas kernels  236 us (98%)
  local copies, waits for them, and re-layouts  2.94 us (1%)
    pallas_call x1, Pallas kernels, head_call(): pl.pallas_call(functools.partial(head_kernel, n), out_shape=(jax.ShapeDty...  227 us
    pallas_call x1, Pallas kernels, passed(): pl.pallas_call(pass_kernel, grid=(rows // size,), out_shape=jax.ShapeDtyp...  8.94 us

profile of v3, /device:TPU:21, one launch (start us, length us, event | category | flops | bytes accessed | tf_op | source)
XLA Modules:
  0.0 242.0 jit_solution(6778473460669031252)
XLA Ops:
  0.6 0.8 stack_reshape.7
  1.4 0.7 convert_element_type.3
  2.1 0.1 stack_reshape.6
  2.2 0.6 pad_maximum_fusion.aux_ref
  2.8 226.9 %head.1 = (bf16[2,256,768]{2,1,0:T(8,128)(2,1)}, f32[768,3200]{1,0:T(8,128)}, f32[768]{0:T(1024)}, f32[768]{0:T(1024)}, f32[1,128]{1,0:T(1,128)}, /*index=5*/f32[32,3200,256]{2,1,0:T(8,128)}) custom-call(bf16[2,256,768]{2,1,0:T(8,128)(2,1)} %bitcast.4, f32[768]{0:T(1024)} %gain_ref.1, f32[768]{0:T(1024)} %bias_ref.1, bf16[768,3200]{1,0:T(8,128)(2,1)} %w_hbm.1, ...), custom_call_target="tpu_custom_call" | custom-call | tf_op jit(solution)/shard_map/head/pallas_call | solution.py:436
  229.7 0.0 copy-start.3
  229.7 0.0 copy-start
  229.7 0.0 copy-start.2
  229.8 0.0 copy-start.1
  229.8 8.9 %passed.1 = f32[768,3200]{1,0:T(8,128)} custom-call(f32[768,3200]{1,0:T(8,128)} %get-tuple-element.12.x_ref), custom_call_target="tpu_custom_call" | custom-call | tf_op jit(solution)/shard_map/passed/pallas_call | solution.py:489
  238.7 0.0 copy-done.3
  238.7 0.0 copy-done
  238.8 0.9 copy.16
  239.6 0.0 copy-done.2
  239.6 0.6 copy.17
  240.2 0.0 copy-done.1
  240.2 0.6 copy.18
Async XLA Ops:
  229.7 9.0 %copy-start.3 = (f32[1,128]{1,0:T(1,128)S(1)}, f32[1,128]{1,0:T(1,128)}, u32[]{:S(2)}) copy-start(f32[1,128]{1,0:T(1,128)} %get-tuple-element.10) | copy-start | bytes 1540
  229.7 9.0 %copy-start = (bf16[2,256,768]{2,1,0:T(8,128)(2,1)S(1)}, bf16[2,256,768]{2,1,0:T(8,128)(2,1)}, u32[]{:S(2)}) copy-start(bf16[2,256,768]{2,1,0:T(8,128)(2,1)} %get-tuple-element.11) | copy-start | bytes 2359300
  229.7 9.9 %copy-start.2 = (f32[768]{0:T(1024)S(1)}, f32[768]{0:T(1024)}, u32[]{:S(2)}) copy-start(f32[768]{0:T(1024)} %get-tuple-element.23) | copy-start | bytes 9220
  229.8 10.5 %copy-start.1 = (f32[768]{0:T(1024)S(1)}, f32[768]{0:T(1024)}, u32[]{:S(2)}) copy-start(f32[768]{0:T(1024)} %get-tuple-element.24) | copy-start | bytes 9220
